TPU v7x, 32 devices: a whole 2x2x4 slice. The times are simulated.
32 devices in a mesh: ctx: 4 (over y, core), fsdp: 2 (over x), head: 4 (over z).
Axes of the slice: x: 2, y: 2, z: 4, core: 2. Of those that a mesh axis runs over, the one named last changes fastest.
Arguments:
- inputs: bfloat16 [4096, 2048], P(('ctx', 'fsdp')), may hold values from -6 to 6
- query_weight: bfloat16 [2048, 2048], P('fsdp', 'head'), may hold values from -0.13258252 to 0.13258252
- key_weight: bfloat16 [2048, 256], P('fsdp', 'head'), may hold values from -0.125 to 0.125
- value_weight: bfloat16 [2048, 256], P('fsdp', 'head'), may hold values from -0.125 to 0.125
- output_weight: bfloat16 [2048, 2048], P('head', 'fsdp'), may hold values from -6 to 6
- gate_weight: bfloat16 [2048, 5632], P('fsdp', 'head'), may hold values from -0.125 to 0.125
- up_weight: bfloat16 [2048, 5632], P('fsdp', 'head'), may hold values from -0.125 to 0.125
- down_weight: bfloat16 [5632, 2048], P('head', 'fsdp'), may hold values from -0.15625 to 0.15625
- attn_gain: bfloat16 [2048], P('fsdp'), may hold values from 0.099609375 to 1.8984375
- ffn_gain: bfloat16 [2048], P('fsdp'), may hold values from 0.099609375 to 1.8984375
- cotangent: bfloat16 [4096, 2048], P(('ctx', 'fsdp')), may hold values from -6 to 6
Outputs:
- outputs: bfloat16 [4096, 2048], P(('ctx', 'fsdp'))
- input_grad: float32 [4096, 2048], P(('ctx', 'fsdp'))
- query_grad: float32 [2048, 2048], P('fsdp', 'head')
- key_grad: float32 [2048, 256], P('fsdp', 'head')
- value_grad: float32 [2048, 256], P('fsdp', 'head')
- output_grad: float32 [2048, 2048], P('head', 'fsdp')
- gate_grad: float32 [2048, 5632], P('fsdp', 'head')
- up_grad: float32 [2048, 5632], P('fsdp', 'head')
- down_grad: float32 [5632, 2048], P('head', 'fsdp')
- attn_gain_grad: float32 [2048], P('fsdp')
- ffn_gain_grad: float32 [2048], P('fsdp')
All inputs are finite; a program needn't handle non-finite values.
Results may differ from a plain program's by a relative error of at most 0.025.
Values may be sent and summed in bfloat16 or wider, within the bound.
A program may use at most 256 MiB of HBM per device.

v0:
```python
import jax
import jax.numpy as jnp
from jax import lax
from jax.sharding import PartitionSpec as P

HEAD_DIM = 64
EPSILON = 1e-05


def rotate(values, positions, inverse):
    half_dim = values.shape[-1] // 2
    freqs = 10000.0 ** (-2.0 * jnp.arange(half_dim, dtype=jnp.float32) / values.shape[-1])
    angles = positions.astype(jnp.float32)[:, None] * freqs[None, :]
    cosine = jnp.cos(angles)[:, None, :]
    sine = jnp.sin(angles)[:, None, :]
    if inverse:
        sine = -sine
    first = values[..., :half_dim]
    second = values[..., half_dim:]
    return jnp.concatenate(
        [first * cosine - second * sine, second * cosine + first * sine], axis=-1
    )


def matmul(left, right):
    return jnp.dot(left, right, preferred_element_type=jnp.float32)


def mat_trans(left, right):
    return lax.dot_general(
        left, right, (((1,), (1,)), ((), ())), preferred_element_type=jnp.float32
    )


def trans_mat(left, right):
    return lax.dot_general(
        left, right, (((0,), (0,)), ((), ())), preferred_element_type=jnp.float32
    )


def shards(
    inputs,
    query_weight,
    key_weight,
    value_weight,
    output_weight,
    gate_weight,
    up_weight,
    down_weight,
    attn_gain,
    ffn_gain,
    cotangent,
):
    local_weights = (
        attn_gain,
        ffn_gain,
        query_weight,
        key_weight,
        value_weight,
        gate_weight,
        up_weight,
        output_weight,
        down_weight,
    )
    full_weights = (
        lax.all_gather(local_weights[0], "fsdp", axis=0, tiled=True),
        lax.all_gather(local_weights[1], "fsdp", axis=0, tiled=True),
        lax.all_gather(local_weights[2], "fsdp", axis=0, tiled=True),
        lax.all_gather(local_weights[3], "fsdp", axis=0, tiled=True),
        lax.all_gather(local_weights[4], "fsdp", axis=0, tiled=True),
        lax.all_gather(local_weights[5], "fsdp", axis=0, tiled=True),
        lax.all_gather(local_weights[6], "fsdp", axis=0, tiled=True),
        lax.all_gather(local_weights[7], "fsdp", axis=1, tiled=True),
        lax.all_gather(local_weights[8], "fsdp", axis=1, tiled=True),
    )
    gain_one, gain_two, w_query, w_key, w_value, w_gate, w_up, w_out, w_down = full_weights
    row_count = inputs.shape[0]
    heads_here = w_query.shape[1] // HEAD_DIM
    positions = lax.axis_index(("ctx", "fsdp")) * row_count + jnp.arange(row_count, dtype=jnp.int32)
    last_pos = positions[row_count - 1]
    seq_total = row_count * lax.axis_size(("ctx", "fsdp"))
    in_float = inputs.astype(jnp.float32)
    scale_one = lax.rsqrt(jnp.mean(in_float * in_float, axis=-1, keepdims=True) + EPSILON)
    unit_one = in_float * scale_one
    normed_one = (unit_one * gain_one.astype(jnp.float32)).astype(jnp.bfloat16)
    queries = (
        (
            rotate(
                matmul(normed_one, w_query).reshape(row_count, heads_here, HEAD_DIM),
                positions,
                False,
            )
            * 0.125
        )
        .astype(jnp.bfloat16)
        .transpose(1, 0, 2)
    )
    keys_mine = (
        rotate(matmul(normed_one, w_key).reshape(row_count, 1, HEAD_DIM), positions, False)
        .reshape(row_count, HEAD_DIM)
        .astype(jnp.bfloat16)
    )
    values_mine = matmul(normed_one, w_value).astype(jnp.bfloat16)
    start_state = (
        jnp.full((heads_here, row_count), -1e30, jnp.float32),
        jnp.zeros((heads_here, row_count), jnp.float32),
        jnp.zeros((heads_here, row_count, HEAD_DIM), jnp.float32),
    )
    key_piece = lax.all_gather(keys_mine, ("ctx", "fsdp"), axis=0, tiled=True)
    value_piece = lax.all_gather(values_mine, ("ctx", "fsdp"), axis=0, tiled=True)

    def attend_block(offset, inner):
        key_start = offset * row_count

        def attend_compute(current):
            running_max, running_sum, running_acc = current
            key_block = lax.dynamic_slice_in_dim(key_piece, offset * row_count, row_count, 0)
            value_block = lax.dynamic_slice_in_dim(value_piece, offset * row_count, row_count, 0)
            scores = jnp.einsum(
                "hrd,kd->hrk", queries, key_block, preferred_element_type=jnp.float32
            )
            allowed = (key_start + jnp.arange(row_count, dtype=jnp.int32))[None, :] <= positions[
                :, None
            ]
            scores = jnp.where(allowed[None], scores, -1e30)
            new_max = jnp.maximum(running_max, jnp.max(scores, axis=-1))
            rescale = jnp.exp(running_max - new_max)
            weights = jnp.where(allowed[None], jnp.exp(scores - new_max[..., None]), 0.0)
            running_sum = running_sum * rescale + jnp.sum(weights, axis=-1)
            running_acc = running_acc * rescale[..., None] + jnp.einsum(
                "hrk,kd->hrd",
                weights.astype(jnp.bfloat16),
                value_block,
                preferred_element_type=jnp.float32,
            )
            return (new_max, running_sum, running_acc)

        return lax.cond(key_start <= last_pos, attend_compute, lambda current: current, inner)

    run_max, run_sum, run_acc = lax.fori_loop(
        0, key_piece.shape[0] // row_count, attend_block, start_state
    )
    log_sums = run_max + jnp.log(run_sum)
    attended = (run_acc / run_sum[..., None]).astype(jnp.bfloat16)
    concat_heads = attended.transpose(1, 0, 2).reshape(row_count, heads_here * HEAD_DIM)
    hidden = in_float + lax.psum(matmul(concat_heads, w_out).astype(jnp.bfloat16), "head").astype(
        jnp.float32
    )
    scale_two = lax.rsqrt(jnp.mean(hidden * hidden, axis=-1, keepdims=True) + EPSILON)
    unit_two = hidden * scale_two
    normed_two = (unit_two * gain_two.astype(jnp.float32)).astype(jnp.bfloat16)
    gate_pre = matmul(normed_two, w_gate)
    up_pre = matmul(normed_two, w_up)
    silu_gate = jax.nn.silu(gate_pre)
    activated = (silu_gate * up_pre).astype(jnp.bfloat16)
    outputs = (
        hidden
        + lax.psum(matmul(activated, w_down).astype(jnp.bfloat16), "head").astype(jnp.float32)
    ).astype(jnp.bfloat16)
    back_weights = (
        lax.all_gather(local_weights[0], "fsdp", axis=0, tiled=True),
        lax.all_gather(local_weights[1], "fsdp", axis=0, tiled=True),
        lax.all_gather(local_weights[2], "fsdp", axis=0, tiled=True),
        lax.all_gather(local_weights[3], "fsdp", axis=0, tiled=True),
        lax.all_gather(local_weights[4], "fsdp", axis=0, tiled=True),
        lax.all_gather(local_weights[5], "fsdp", axis=0, tiled=True),
        lax.all_gather(local_weights[6], "fsdp", axis=0, tiled=True),
        lax.all_gather(local_weights[7], "fsdp", axis=1, tiled=True),
        lax.all_gather(local_weights[8], "fsdp", axis=1, tiled=True),
    )
    gain_one, gain_two, w_query, w_key, w_value, w_gate, w_up, w_out, w_down = back_weights
    out_float = cotangent.astype(jnp.float32)
    act_grad = mat_trans(cotangent, w_down)
    down_part = trans_mat(activated, cotangent)
    sigma = jax.nn.sigmoid(gate_pre)
    gate_in_grad = (act_grad * up_pre * sigma * (1.0 + gate_pre * (1.0 - sigma))).astype(
        jnp.bfloat16
    )
    up_in_grad = (act_grad * silu_gate).astype(jnp.bfloat16)
    gate_part = trans_mat(normed_two, gate_in_grad)
    up_part = trans_mat(normed_two, up_in_grad)
    normed_two_grad = lax.psum(
        (mat_trans(gate_in_grad, w_gate) + mat_trans(up_in_grad, w_up)).astype(jnp.bfloat16), "head"
    ).astype(jnp.float32)
    gain_two_part = jnp.sum(normed_two_grad * unit_two, axis=0)
    scaled_two = normed_two_grad * gain_two.astype(jnp.float32)
    hidden_grad = out_float + scale_two * (
        scaled_two - unit_two * jnp.mean(scaled_two * unit_two, axis=-1, keepdims=True)
    )
    hidden_low = hidden_grad.astype(jnp.bfloat16)
    out_part = trans_mat(concat_heads, hidden_low)
    attended_grad = mat_trans(hidden_low, w_out).astype(jnp.bfloat16)
    grad_heads = attended_grad.reshape(row_count, heads_here, HEAD_DIM).transpose(1, 0, 2)
    deltas = jnp.sum(grad_heads.astype(jnp.float32) * attended.astype(jnp.float32), axis=-1)
    back_state = (
        jnp.zeros((heads_here, row_count, HEAD_DIM), jnp.float32),
        jnp.zeros((seq_total, 2 * HEAD_DIM), jnp.float32),
    )
    back_key_piece = lax.all_gather(keys_mine, ("ctx", "fsdp"), axis=0, tiled=True)
    back_value_piece = lax.all_gather(values_mine, ("ctx", "fsdp"), axis=0, tiled=True)

    def back_block(offset, inner):
        key_start = offset * row_count

        def back_compute(current):
            query_acc, pair_acc = current
            key_block = lax.dynamic_slice_in_dim(back_key_piece, offset * row_count, row_count, 0)
            value_block = lax.dynamic_slice_in_dim(
                back_value_piece, offset * row_count, row_count, 0
            )
            scores = jnp.einsum(
                "hrd,kd->hrk", queries, key_block, preferred_element_type=jnp.float32
            )
            allowed = (key_start + jnp.arange(row_count, dtype=jnp.int32))[None, :] <= positions[
                :, None
            ]
            scores = jnp.where(allowed[None], scores, -1e30)
            probs = jnp.where(allowed[None], jnp.exp(scores - log_sums[..., None]), 0.0)
            prob_grad = jnp.einsum(
                "hrd,kd->hrk", grad_heads, value_block, preferred_element_type=jnp.float32
            )
            score_grad = (probs * (prob_grad - deltas[..., None])).astype(jnp.bfloat16)
            query_acc = query_acc + jnp.einsum(
                "hrk,kd->hrd", score_grad, key_block, preferred_element_type=jnp.float32
            )
            key_part = jnp.einsum(
                "hrk,hrd->kd", score_grad, queries, preferred_element_type=jnp.float32
            )
            value_part = jnp.einsum(
                "hrk,hrd->kd",
                probs.astype(jnp.bfloat16),
                grad_heads,
                preferred_element_type=jnp.float32,
            )
            rows_now = lax.dynamic_slice_in_dim(pair_acc, key_start, row_count, 0)
            pair_acc = lax.dynamic_update_slice_in_dim(
                pair_acc, rows_now + jnp.concatenate([key_part, value_part], axis=1), key_start, 0
            )
            return (query_acc, pair_acc)

        return lax.cond(key_start <= last_pos, back_compute, lambda current: current, inner)

    query_acc, pair_acc = lax.fori_loop(
        0, back_key_piece.shape[0] // row_count, back_block, back_state
    )
    pair_mine = lax.psum_scatter(
        pair_acc.astype(jnp.bfloat16), ("ctx", "fsdp"), scatter_dimension=0, tiled=True
    ).astype(jnp.float32)
    q_raw = (
        rotate((query_acc * 0.125).transpose(1, 0, 2), positions, True)
        .reshape(row_count, heads_here * HEAD_DIM)
        .astype(jnp.bfloat16)
    )
    k_raw = (
        rotate(pair_mine[:, :HEAD_DIM].reshape(row_count, 1, HEAD_DIM), positions, True)
        .reshape(row_count, HEAD_DIM)
        .astype(jnp.bfloat16)
    )
    v_raw = pair_mine[:, HEAD_DIM:].astype(jnp.bfloat16)
    query_part = trans_mat(normed_one, q_raw)
    key_part_w = trans_mat(normed_one, k_raw)
    value_part_w = trans_mat(normed_one, v_raw)
    normed_one_grad = lax.psum(
        (mat_trans(q_raw, w_query) + mat_trans(k_raw, w_key) + mat_trans(v_raw, w_value)).astype(
            jnp.bfloat16
        ),
        "head",
    ).astype(jnp.float32)
    gain_one_part = jnp.sum(normed_one_grad * unit_one, axis=0)
    scaled_one = normed_one_grad * gain_one.astype(jnp.float32)
    input_grad = hidden_grad + scale_one * (
        scaled_one - unit_one * jnp.mean(scaled_one * unit_one, axis=-1, keepdims=True)
    )
    grad_terms = (
        gain_one_part,
        gain_two_part,
        query_part,
        key_part_w,
        value_part_w,
        gate_part,
        up_part,
        out_part,
        down_part,
    )
    grad_halves = (
        lax.psum_scatter(
            grad_terms[0].astype(jnp.bfloat16), "fsdp", scatter_dimension=0, tiled=True
        ).astype(jnp.float32),
        lax.psum_scatter(
            grad_terms[1].astype(jnp.bfloat16), "fsdp", scatter_dimension=0, tiled=True
        ).astype(jnp.float32),
        lax.psum_scatter(
            grad_terms[2].astype(jnp.bfloat16), "fsdp", scatter_dimension=0, tiled=True
        ).astype(jnp.float32),
        lax.psum_scatter(
            grad_terms[3].astype(jnp.bfloat16), "fsdp", scatter_dimension=0, tiled=True
        ).astype(jnp.float32),
        lax.psum_scatter(
            grad_terms[4].astype(jnp.bfloat16), "fsdp", scatter_dimension=0, tiled=True
        ).astype(jnp.float32),
        lax.psum_scatter(
            grad_terms[5].astype(jnp.bfloat16), "fsdp", scatter_dimension=0, tiled=True
        ).astype(jnp.float32),
        lax.psum_scatter(
            grad_terms[6].astype(jnp.bfloat16), "fsdp", scatter_dimension=0, tiled=True
        ).astype(jnp.float32),
        lax.psum_scatter(
            grad_terms[7].astype(jnp.bfloat16), "fsdp", scatter_dimension=1, tiled=True
        ).astype(jnp.float32),
        lax.psum_scatter(
            grad_terms[8].astype(jnp.bfloat16), "fsdp", scatter_dimension=1, tiled=True
        ).astype(jnp.float32),
    )
    summed = (
        lax.psum(grad_halves[0].astype(jnp.bfloat16), "ctx").astype(jnp.float32),
        lax.psum(grad_halves[1].astype(jnp.bfloat16), "ctx").astype(jnp.float32),
        lax.psum(grad_halves[2].astype(jnp.bfloat16), "ctx").astype(jnp.float32),
        lax.psum(grad_halves[3].astype(jnp.bfloat16), "ctx").astype(jnp.float32),
        lax.psum(grad_halves[4].astype(jnp.bfloat16), "ctx").astype(jnp.float32),
        lax.psum(grad_halves[5].astype(jnp.bfloat16), "ctx").astype(jnp.float32),
        lax.psum(grad_halves[6].astype(jnp.bfloat16), "ctx").astype(jnp.float32),
        lax.psum(grad_halves[7].astype(jnp.bfloat16), "ctx").astype(jnp.float32),
        lax.psum(grad_halves[8].astype(jnp.bfloat16), "ctx").astype(jnp.float32),
    )
    (
        gain_one_grad,
        gain_two_grad,
        query_grad,
        key_grad,
        value_grad,
        gate_grad,
        up_grad,
        output_grad,
        down_grad,
    ) = summed
    return (
        outputs,
        input_grad,
        query_grad,
        key_grad,
        value_grad,
        output_grad,
        gate_grad,
        up_grad,
        down_grad,
        gain_one_grad,
        gain_two_grad,
    )


def solution(mesh):
    return jax.shard_map(
        shards,
        mesh=mesh,
        in_specs=(
            P(("ctx", "fsdp"), None),
            P("fsdp", "head"),
            P("fsdp", "head"),
            P("fsdp", "head"),
            P("head", "fsdp"),
            P("fsdp", "head"),
            P("fsdp", "head"),
            P("head", "fsdp"),
            P("fsdp"),
            P("fsdp"),
            P(("ctx", "fsdp"), None),
        ),
        out_specs=(
            P(("ctx", "fsdp"), None),
            P(("ctx", "fsdp"), None),
            P("fsdp", "head"),
            P("fsdp", "head"),
            P("fsdp", "head"),
            P("head", "fsdp"),
            P("fsdp", "head"),
            P("fsdp", "head"),
            P("head", "fsdp"),
            P("fsdp"),
            P("fsdp"),
        ),
        check_vma=False,
    )
```

profile of v0, /device:TPU:0, one launch (start us, length us, event | category | flops | bytes accessed | tf_op | source)
XLA Modules:
  0.0 1465.6 jit_solution(13294570087655459204)
XLA Ops:
  16.4 7.5 all_gather.45
  23.9 9.0 all_gather.48
  35.2 18.7 %all-gather = bf16[4096,1,64]{0,2,1:T(8,128)(2,1)S(1)} all-gather(bf16[512,1,64]{0,2,1:T(8,128)(2,1)S(1)} %pad_maximum_fusion.1), channel_id=2, replica_groups=mesh['ctx'=4,'fsdp'=2,'head'=4] {'ctx','fsdp'}, dimensions={0}, use_global_device_ids=true | all-gather | bytes 589824 | tf_op jit(solution)/shard_map/all_gather | solution.py:109
  54.7 21.4 %all_gather.49 = bf16[4096,64]{0,1:T(8,128)(2,1)} all-gather(bf16[512,64]{0,1:T(8,128)(2,1)S(1)} %convolution_convert_fusion.10), channel_id=1, replica_groups=mesh['ctx'=4,'fsdp'=2,'head'=4] {'ctx','fsdp'}, dimensions={0}, use_global_device_ids=true | all-gather | bytes 589824 | tf_op jit(solution)/shard_map/all_gather | solution.py:110
  82.0 12.6 while.34
  82.5 7.7 conditional.6
  102.9 11.6 all_gather.51
  114.5 127.7 %all-reduce.11.cloned.1.call-done = bf16[512,2048]{1,0:T(8,128)(2,1)} async-done(((bf16[512,2048]{1,0:T(8,128)(2,1)}), bf16[512,2048]{1,0:T(8,128)(2,1)}) %all-reduce.11.cloned.1.call-update) | async-done | bytes 2097168 | tf_op jit(solution)/shard_map/psum | solution.py:146
  247.1 70.0 %all-gather.11.cloned.1.call-done = bf16[2048,1408]{1,0:T(8,128)(2,1)} async-done(((bf16[1024,1408]{1,0:T(8,128)(2,1)}), bf16[2048,1408]{1,0:T(8,128)(2,1)}) %all-gather.11.cloned.1.call-update) | async-done | bytes 5767184 | tf_op jit(solution)/shard_map/all_gather | solution.py:71
  317.1 8.3 fusion.97
  325.4 67.6 %all-gather.13.cloned.1.call-done = bf16[2048,1408]{1,0:T(8,128)(2,1)} async-done(((bf16[1024,1408]{1,0:T(8,128)(2,1)}), bf16[2048,1408]{1,0:T(8,128)(2,1)}) %all-gather.13.cloned.1.call-update) | async-done | bytes 5767184 | tf_op jit(solution)/shard_map/all_gather | solution.py:72
  393.0 8.3 fusion.98
  401.2 67.6 %all-gather.15.cloned.1.call-done = bf16[1408,2048]{1,0:T(8,128)(2,1)} async-done(((bf16[1408,1024]{1,0:T(8,128)(2,1)}), bf16[1408,2048]{1,0:T(8,128)(2,1)}) %all-gather.15.cloned.1.call-update) | async-done | bytes 5767184 | tf_op jit(solution)/shard_map/all_gather | solution.py:74
  468.9 10.4 multiply_convert_fusion.1
  479.2 6.6 fusion.99
  491.0 85.8 %all-reduce.13.cloned.1.call-done = bf16[512,2048]{1,0:T(8,128)(2,1)} async-done(((bf16[512,2048]{1,0:T(8,128)(2,1)}), bf16[512,2048]{1,0:T(8,128)(2,1)}) %all-reduce.13.cloned.1.call-update) | async-done | bytes 2097168 | tf_op jit(solution)/shard_map/psum | solution.py:182
  588.3 21.8 %while.35 = (s32[]{:T(128)}, f32[8,512,64]{1,2,0:T(8,128)}, f32[4096,128]{0,1:T(8,128)}, s32[]{:T(128)}, bf16[4096,64]{0,1:T(8,128)(2,1)S(1)}, /*index=5*/bf16[8...) while((s32[]{:T(128)}, f32[8,512,64]{1,2,0:T(8,128)}, ...), condition=%wide.region_16.17_spmd.clone, body=%wide.region_13.0_spmd.clone.sunk | while | flops 1363805184 | bytes 62910912 | solution.py:243
  588.9 16.9 %conditional.7 = ((f32[8,512,64]{1,2,0:T(8,128)}, f32[4096,128]{0,1:T(8,128)})) conditional(s32[]{:T(128)} %convert_element_type.413, (f32[8,512,64]{1,2,0:T(8,128)}, f32[4096,128]{0,1:T(8,128)}) %tuple.101, (s32[]{:T(128)}, s32[]{:T(128)}, s32[]{:T(128)}, bf16[4096,64]{0,1:T(8,128)(2,1)S(1)}, bf16[8,512,64]{1,2,0:T(8,128)(2,1)S(1)}, ...), branch_computations={%region_14.14_spmd, %region_15.15_spmd} | conditional | flops 1363805184 | bytes 62908600 | solution.py:241
  612.9 152.7 %reduce-scatter.9.cloned.1.call-done = bf16[512,128]{0,1:T(8,128)(2,1)} async-done(((bf16[4096,128]{0,1:T(8,128)(2,1)}), bf16[512,128]{0,1:T(8,128)(2,1)}) %reduce-scatter.9.cloned.1.call-update) | async-done | bytes 131088 | tf_op jit(solution)/shard_map/reduce_scatter | solution.py:246
  783.7 8.0 convolution_convert_fusion.2
  791.8 8.0 convolution_convert_fusion.1
  800.1 7.8 convolution_convert_fusion
  807.9 8.0 convolution_convert_fusion.6
  820.4 9.8 reduce-scatter.17.cloned.1.call-done
  830.2 34.6 %reduce-scatter.11.cloned.1.call-done = bf16[1024,512]{1,0:T(8,128)(2,1)} async-done(((bf16[2048,512]{1,0:T(8,128)(2,1)}), bf16[1024,512]{1,0:T(8,128)(2,1)}) %reduce-scatter.11.cloned.1.call-update) | async-done | bytes 1048592 | tf_op jit(solution)/shard_map/reduce_scatter | solution.py:292
  864.8 74.3 %reduce-scatter.19.cloned.1.call-done = bf16[1024,1408]{1,0:T(8,128)(2,1)} async-done(((bf16[2048,1408]{1,0:T(8,128)(2,1)}), bf16[1024,1408]{1,0:T(8,128)(2,1)}) %reduce-scatter.19.cloned.1.call-update) | async-done | bytes 2883600 | tf_op jit(solution)/shard_map/reduce_scatter | solution.py:301
  939.1 74.2 %reduce-scatter.21.cloned.1.call-done = bf16[1024,1408]{1,0:T(8,128)(2,1)} async-done(((bf16[2048,1408]{1,0:T(8,128)(2,1)}), bf16[1024,1408]{1,0:T(8,128)(2,1)}) %reduce-scatter.21.cloned.1.call-update) | async-done | bytes 2883600 | tf_op jit(solution)/shard_map/reduce_scatter | solution.py:304
  1013.3 74.2 %reduce-scatter.23.cloned.1.call-done = bf16[1408,1024]{1,0:T(8,128)(2,1)} async-done(((bf16[1408,2048]{1,0:T(8,128)(2,1)}), bf16[1408,1024]{1,0:T(8,128)(2,1)}) %reduce-scatter.23.cloned.1.call-update) | async-done | bytes 2883600 | tf_op jit(solution)/shard_map/reduce_scatter | solution.py:310
  1089.4 156.0 %all-reduce.15.cloned.1.call-done = (bf16[512,2048]{1,0:T(8,128)(2,1)}, bf16[512,2048]{1,0:T(8,128)(2,1)}) async-done(((bf16[512,2048]{1,0:T(8,128)(2,1)}, bf16[512,2048]{1,0:T(8,128)(2,1)}), (bf16[512,2048]{1,0:T(8,128)(2,1)}, bf16[512,2048]{1,0:T(8,128)(2,1)})) %all-reduce.15.cloned.1.call-update) | async-done | bytes 4194320 | tf_op jit(solution)/shard_map/psum | solution.py:158
  1253.4 6.7 all-reduce.3
  1261.3 7.8 fusion.54
  1269.2 173.9 %all-reduce.17.cloned.1.call-done = (bf16[1024,512]{1,0:T(8,128)(2,1)}, bf16[1024,64]{0,1:T(8,128)(2,1)}, bf16[1024,64]{0,1:T(8,128)(2,1)}, bf16[512,1024]{1,0:T...) async-done(((bf16[1024,512]{1,0:T(8,128)(2,1)}, bf16[1024,64]{0,1:T(8,128)(2,1)}, bf16[1024,64]{0,1:T(8,128)(2,1)}, ...) | async-done | bytes 11010064 | tf_op jit(solution)/shard_map/psum | solution.py:317
  (229 shorter events, 124.0 us)
Async XLA Ops:
  7.2 26.3 %copy-start.1 = (bf16[512,2048]{1,0:T(8,128)(2,1)S(1)}, bf16[512,2048]{1,0:T(8,128)(2,1)}, u32[]{:S(2)}) copy-start(bf16[512,2048]{1,0:T(8,128)(2,1)} %param.19) | copy-start | bytes 6291460
  7.2 9.2 copy-start.26
  7.2 16.7 %copy-start.27 = (bf16[1024,64]{0,1:T(8,128)(2,1)S(1)}, bf16[1024,64]{0,1:T(8,128)(2,1)}, u32[]{:S(2)}) copy-start(bf16[1024,64]{0,1:T(8,128)(2,1)} %param.22) | copy-start | bytes 393220
  7.2 69.8 %all-gather.7.cloned.1.call-start = ((), (), s32[]{:S(2)}) async-start(), calls=%async_computation.8 | async-start | bytes 3145728 | tf_op jit(solution)/shard_map/all_gather | solution.py:68
  7.9 88.8 %all-gather.9.cloned.1.call-start = ((), (), s32[]{:S(2)}) async-start(), calls=%async_computation.9 | async-start | bytes 3145728 | tf_op jit(solution)/shard_map/all_gather | solution.py:73
  8.7 233.5 %all-reduce.11.cloned.1.call-start = ((), (), s32[]{:S(2)}) async-start(), calls=%async_computation.10 | async-start | bytes 4194304 | tf_op jit(solution)/shard_map/psum | solution.py:146
  8.8 67.3 %copy-start.34 = (f32[32]{0:T(128)}, f32[32]{0:T(128)S(1)}, u32[]{:S(2)}) copy-start(f32[32]{0:T(128)S(1)} %multiply_power_fusion) | copy-start | bytes 388
  8.8 67.3 %copy-start.30 = (f32[512]{0:T(512)}, f32[512]{0:T(512)S(1)}, u32[]{:S(2)}) copy-start(f32[512]{0:T(512)S(1)} %fusion.91) | copy-start | bytes 6148
  14.3 20.5 %copy-start.24 = (f32[2048]{0:T(1024)}, f32[2048]{0:T(1024)S(1)}, u32[]{:S(2)}) copy-start(f32[2048]{0:T(1024)S(1)} %convert_element_type.200) | copy-start | bytes 24580
  16.4 18.8 %copy-start.32 = (f32[512]{0:T(512)}, f32[512]{0:T(512)S(1)}, u32[]{:S(2)}) copy-start(f32[512]{0:T(512)S(1)} %add_rsqrt_fusion.1) | copy-start | bytes 6148
  23.9 30.8 %copy-start.12 = (bf16[2048,64]{0,1:T(8,128)(2,1)}, bf16[2048,64]{0,1:T(8,128)(2,1)S(1)}, u32[]{:S(2)}) copy-start(bf16[2048,64]{0,1:T(8,128)(2,1)S(1)} %all_gather.45) | copy-start | bytes 786436
  32.9 21.8 %copy-start.14 = (bf16[2048,64]{0,1:T(8,128)(2,1)}, bf16[2048,64]{0,1:T(8,128)(2,1)S(1)}, u32[]{:S(2)}) copy-start(bf16[2048,64]{0,1:T(8,128)(2,1)S(1)} %all_gather.48) | copy-start | bytes 786436
  34.1 19.9 %copy-start.2 = (bf16[512,2048]{1,0:T(8,128)(2,1)}, bf16[512,2048]{1,0:T(8,128)(2,1)S(1)}, u32[]{:S(2)}) copy-start(bf16[512,2048]{1,0:T(8,128)(2,1)S(1)} %fusion.59) | copy-start | bytes 6291460
  101.1 216.0 %all-gather.11.cloned.1.call-start = ((), (), s32[]{:S(2)}) async-start(), calls=%async_computation.11 | async-start | bytes 8650752 | tf_op jit(solution)/shard_map/all_gather | solution.py:71
  101.7 291.3 %all-gather.13.cloned.1.call-start = ((), (), s32[]{:S(2)}) async-start(), calls=%async_computation.12 | async-start | bytes 8650752 | tf_op jit(solution)/shard_map/all_gather | solution.py:72
  102.3 366.6 %all-gather.15.cloned.1.call-start = ((), (), s32[]{:S(2)}) async-start(), calls=%async_computation.13 | async-start | bytes 8650752 | tf_op jit(solution)/shard_map/all_gather | solution.py:74
  102.9 474.0 %all-reduce.13.cloned.1.call-start = ((), (), s32[]{:S(2)}) async-start(), calls=%async_computation.14 | async-start | bytes 4194304 | tf_op jit(solution)/shard_map/psum | solution.py:182
  490.5 275.1 %reduce-scatter.9.cloned.1.call-start = ((), (), s32[]{:S(2)}) async-start(), calls=%async_computation.15 | async-start | bytes 1179648 | tf_op jit(solution)/shard_map/reduce_scatter | solution.py:246
  610.1 156.3 %copy-start.31 = (f32[512]{0:T(512)S(1)}, f32[512]{0:T(512)}, u32[]{:S(2)}) copy-start(f32[512]{0:T(512)} %copy-done.30) | copy-start | bytes 6148
  610.1 156.3 %copy-start.35 = (f32[32]{0:T(128)S(1)}, f32[32]{0:T(128)}, u32[]{:S(2)}) copy-start(f32[32]{0:T(128)} %copy-done.34) | copy-start | bytes 388
  612.8 207.5 %reduce-scatter.13.cloned.1.call-start = ((), (), s32[]{:S(2)}) async-start(), calls=%async_computation.17 | async-start | bytes 393216 | tf_op jit(solution)/shard_map/reduce_scatter | solution.py:295
  769.6 50.8 %reduce-scatter.15.cloned.1.call-start = ((), (), s32[]{:S(2)}) async-start(), calls=%async_computation.18 | async-start | bytes 393216 | tf_op jit(solution)/shard_map/reduce_scatter | solution.py:298
  772.5 57.7 %reduce-scatter.17.cloned.1.call-start = ((), (), s32[]{:S(2)}) async-start(), calls=%async_computation.19 | async-start | bytes 3145728 | tf_op jit(solution)/shard_map/reduce_scatter | solution.py:307
  779.3 85.5 %reduce-scatter.11.cloned.1.call-start = ((), (), s32[]{:S(2)}) async-start(), calls=%async_computation.16 | async-start | bytes 3145728 | tf_op jit(solution)/shard_map/reduce_scatter | solution.py:292
  783.7 155.4 %reduce-scatter.19.cloned.1.call-start = ((), (), s32[]{:S(2)}) async-start(), calls=%async_computation.20 | async-start | bytes 8650752 | tf_op jit(solution)/shard_map/reduce_scatter | solution.py:301
  791.8 221.6 %reduce-scatter.21.cloned.1.call-start = ((), (), s32[]{:S(2)}) async-start(), calls=%async_computation.21 | async-start | bytes 8650752 | tf_op jit(solution)/shard_map/reduce_scatter | solution.py:304
  799.8 287.7 %reduce-scatter.23.cloned.1.call-start = ((), (), s32[]{:S(2)}) async-start(), calls=%async_computation.22 | async-start | bytes 8650752 | tf_op jit(solution)/shard_map/reduce_scatter | solution.py:310
  807.9 437.6 %all-reduce.15.cloned.1.call-start = ((), (), s32[]{:S(2)}) async-start(), calls=%async_computation.23 | async-start | bytes 8388608 | tf_op jit(solution)/shard_map/psum | solution.py:158
  807.9 8.0 copy-start.17
  820.3 622.8 %all-reduce.17.cloned.1.call-start = ((), (), s32[]{:S(2)}) async-start(), calls=%async_computation.24 | async-start | bytes 22020096 | tf_op jit(solution)/shard_map/psum | solution.py:317
  1087.6 157.9 %copy-start.25 = (f32[2048]{0:T(1024)S(1)}, f32[2048]{0:T(1024)}, u32[]{:S(2)}) copy-start(f32[2048]{0:T(1024)} %copy-done.24) | copy-start | bytes 24580
  1087.6 157.9 %copy-start.33 = (f32[512]{0:T(512)S(1)}, f32[512]{0:T(512)}, u32[]{:S(2)}) copy-start(f32[512]{0:T(512)} %copy-done.32) | copy-start | bytes 6148
  (27 other events, 83.2 us)
Sparse Core Ops, SparseCore 0:
  9.6 40.0 all-gather.6
  51.2 36.7 all-gather.8
  101.2 140.9 all-reduce.10
  243.6 73.4 all-gather.10
  318.5 74.4 all-gather.12
  394.4 74.4 all-gather.14
  490.6 86.1 all-reduce.12
  613.0 152.5 reduce-scatter.8
  769.7 11.7 reduce-scatter.12
  783.6 11.7 reduce-scatter.14
  798.2 31.9 reduce-scatter.16
  832.8 31.8 reduce-scatter.10
  867.7 71.4 reduce-scatter.18
  941.9 71.4 reduce-scatter.20
  1016.0 71.4 reduce-scatter.22
  1090.4 154.9 all-reduce.14
  1248.5 194.4 all-reduce.16
where the time goes:
time: 1470 us
  waiting for transfers between devices  1170 us (80%)
  matrix products  120 us (8%)
  blocking collectives  85.4 us (6%)
  other arithmetic  50.8 us (3%)
  between operations  15.4 us (1%)
    psum x1, waiting for transfers between devices, shards(): lax.psum(grad_halves[2].astype(jnp.bfloat16), 'ctx').astype(jnp.float32)  174 us
    psum x1, waiting for transfers between devices, shards(): lax.psum(matmul(activated, w_down).astype(jnp.bfloat16), 'head')  156 us
    reduce_scatter x1, waiting for transfers between devices, shards(): lax.psum_scatter(pair_acc.astype(jnp.bfloat16), ('ctx', 'fsdp'), scatter_...  153 us
    psum x1, waiting for transfers between devices, shards(): lax.psum(matmul(concat_heads, w_out).astype(jnp.bfloat16), 'head')  128 us
    psum x1, waiting for transfers between devices, shards(): lax.psum((mat_trans(gate_in_grad, w_gate) + mat_trans(up_in_grad, w_up))....  85.8 us
    reduce_scatter x1, waiting for transfers between devices, shards(): lax.psum_scatter(grad_terms[5].astype(jnp.bfloat16), 'fsdp', scatter_dime...  74.3 us
    reduce_scatter x1, waiting for transfers between devices, shards(): lax.psum_scatter(grad_terms[8].astype(jnp.bfloat16), 'fsdp', scatter_dime...  74.2 us
    reduce_scatter x1, waiting for transfers between devices, shards(): lax.psum_scatter(grad_terms[6].astype(jnp.bfloat16), 'fsdp', scatter_dime...  74.2 us
  transfers between devices with their start and end apart: 17, of which 13 were waited for; matrix products, arithmetic and copies ran while one was open for 7% of the time, Pallas kernels for 0%

commit v1 on v0

--- a/solution.py
+++ b/solution.py
@@ -143,9 +143,9 @@
     log_sums = run_max + jnp.log(run_sum)
     attended = (run_acc / run_sum[..., None]).astype(jnp.bfloat16)
     concat_heads = attended.transpose(1, 0, 2).reshape(row_count, heads_here * HEAD_DIM)
-    hidden = in_float + lax.psum(matmul(concat_heads, w_out).astype(jnp.bfloat16), "head").astype(
-        jnp.float32
-    )
+    hidden = in_float + jnp.sum(
+        lax.all_gather(matmul(concat_heads, w_out).astype(jnp.bfloat16), "head"), axis=0
+    ).astype(jnp.float32)
     scale_two = lax.rsqrt(jnp.mean(hidden * hidden, axis=-1, keepdims=True) + EPSILON)
     unit_two = hidden * scale_two
     normed_two = (unit_two * gain_two.astype(jnp.float32)).astype(jnp.bfloat16)

time: 1470 us -> 1530 us (1.041)
  waiting for transfers between devices: 1170 us -> 1230 us
    all_gather x0 -> x1, waiting for transfers between devices: none -> 191 us  [shards(): lax.all_gather(matmul(concat_heads, w_out).astype(jnp.bfloat16), 'head')]
    psum x1 -> x0, waiting for transfers between devices: 128 us -> none  [shards(): lax.psum(matmul(concat_heads, w_out).astype(jnp.bfloat16), 'head')]
where the time goes in v1:
time: 1530 us
  waiting for transfers between devices  1230 us (80%)
  matrix products  121 us (8%)
  blocking collectives  85.7 us (6%)
  other arithmetic  58.3 us (4%)
  between operations  15.3 us (1%)
    all_gather x1, waiting for transfers between devices, shards(): lax.all_gather(matmul(concat_heads, w_out).astype(jnp.bfloat16), 'head')  191 us
    psum x1, waiting for transfers between devices, shards(): lax.psum(grad_halves[2].astype(jnp.bfloat16), 'ctx').astype(jnp.float32)  174 us
    psum x1, waiting for transfers between devices, shards(): lax.psum(matmul(activated, w_down).astype(jnp.bfloat16), 'head')  156 us
    reduce_scatter x1, waiting for transfers between devices, shards(): lax.psum_scatter(pair_acc.astype(jnp.bfloat16), ('ctx', 'fsdp'), scatter_...  153 us
    psum x1, waiting for transfers between devices, shards(): lax.psum((mat_trans(gate_in_grad, w_gate) + mat_trans(up_in_grad, w_up))....  86.2 us
    reduce_scatter x1, waiting for transfers between devices, shards(): lax.psum_scatter(grad_terms[5].astype(jnp.bfloat16), 'fsdp', scatter_dime...  74.4 us
    reduce_scatter x1, waiting for transfers between devices, shards(): lax.psum_scatter(grad_terms[8].astype(jnp.bfloat16), 'fsdp', scatter_dime...  74.2 us
    reduce_scatter x1, waiting for transfers between devices, shards(): lax.psum_scatter(grad_terms[6].astype(jnp.bfloat16), 'fsdp', scatter_dime...  74.2 us
  transfers between devices with their start and end apart: 17, of which 13 were waited for; matrix products, arithmetic and copies ran while one was open for 7% of the time, Pallas kernels for 0%

profile of v1, /device:TPU:0, one launch (start us, length us, event | category | flops | bytes accessed | tf_op | source)
XLA Modules:
  0.0 1529.2 jit_solution(17703315230951473298)
XLA Ops:
  16.4 7.5 all_gather.51
  23.9 9.0 all_gather.54
  35.3 18.7 %all-gather = bf16[4096,1,64]{0,2,1:T(8,128)(2,1)S(1)} all-gather(bf16[512,1,64]{0,2,1:T(8,128)(2,1)S(1)} %pad_maximum_fusion.1), channel_id=2, replica_groups=mesh['ctx'=4,'fsdp'=2,'head'=4] {'ctx','fsdp'}, dimensions={0}, use_global_device_ids=true | all-gather | bytes 589824 | tf_op jit(solution)/shard_map/all_gather | solution.py:109
  54.8 21.4 %all_gather.55 = bf16[4096,64]{0,1:T(8,128)(2,1)} all-gather(bf16[512,64]{0,1:T(8,128)(2,1)S(1)} %convolution_convert_fusion.10), channel_id=1, replica_groups=mesh['ctx'=4,'fsdp'=2,'head'=4] {'ctx','fsdp'}, dimensions={0}, use_global_device_ids=true | all-gather | bytes 589824 | tf_op jit(solution)/shard_map/all_gather | solution.py:110
  82.1 13.1 while.34
  82.8 7.7 conditional.6
  103.6 11.8 all_gather.59
  115.4 191.0 %all-gather.19.cloned.1.call-done = bf16[2048,2048]{1,0:T(8,128)(2,1)} async-done(((bf16[512,2048]{1,0:T(8,128)(2,1)}), bf16[2048,2048]{1,0:T(8,128)(2,1)}) %all-gather.19.cloned.1.call-update) | async-done | bytes 8388624 | tf_op jit(solution)/shard_map/all_gather | solution.py:147
  306.4 7.2 reduce_sum.85
  318.9 61.6 %all-gather.13.cloned.1.call-done = bf16[2048,1408]{1,0:T(8,128)(2,1)} async-done(((bf16[1024,1408]{1,0:T(8,128)(2,1)}), bf16[2048,1408]{1,0:T(8,128)(2,1)}) %all-gather.13.cloned.1.call-update) | async-done | bytes 5767184 | tf_op jit(solution)/shard_map/all_gather | solution.py:71
  380.4 8.3 fusion.97
  388.7 67.6 %all-gather.15.cloned.1.call-done = bf16[2048,1408]{1,0:T(8,128)(2,1)} async-done(((bf16[1024,1408]{1,0:T(8,128)(2,1)}), bf16[2048,1408]{1,0:T(8,128)(2,1)}) %all-gather.15.cloned.1.call-update) | async-done | bytes 5767184 | tf_op jit(solution)/shard_map/all_gather | solution.py:72
  456.3 8.3 fusion.98
  464.5 67.6 %all-gather.17.cloned.1.call-done = bf16[1408,2048]{1,0:T(8,128)(2,1)} async-done(((bf16[1408,1024]{1,0:T(8,128)(2,1)}), bf16[1408,2048]{1,0:T(8,128)(2,1)}) %all-gather.17.cloned.1.call-update) | async-done | bytes 5767184 | tf_op jit(solution)/shard_map/all_gather | solution.py:74
  532.2 10.4 multiply_convert_fusion.1
  542.5 6.8 fusion.99
  554.1 86.2 %all-reduce.10.cloned.1.call-done = bf16[512,2048]{1,0:T(8,128)(2,1)} async-done(((bf16[512,2048]{1,0:T(8,128)(2,1)}), bf16[512,2048]{1,0:T(8,128)(2,1)}) %all-reduce.10.cloned.1.call-update) | async-done | bytes 2097168 | tf_op jit(solution)/shard_map/psum | solution.py:182
  651.8 22.3 %while.35 = (s32[]{:T(128)}, f32[8,512,64]{1,2,0:T(8,128)}, f32[4096,128]{0,1:T(8,128)}, s32[]{:T(128)}, bf16[4096,64]{0,1:T(8,128)(2,1)S(1)}, /*index=5*/bf16[8...) while((s32[]{:T(128)}, f32[8,512,64]{1,2,0:T(8,128)}, ...), condition=%wide.region_16.17_spmd.clone, body=%wide.region_13.0_spmd.clone.sunk | while | flops 1363805184 | bytes 62910912 | solution.py:243
  652.5 16.9 %conditional.7 = ((f32[8,512,64]{1,2,0:T(8,128)}, f32[4096,128]{0,1:T(8,128)})) conditional(s32[]{:T(128)} %convert_element_type.415, (f32[8,512,64]{1,2,0:T(8,128)}, f32[4096,128]{0,1:T(8,128)}) %tuple.101, (s32[]{:T(128)}, s32[]{:T(128)}, s32[]{:T(128)}, bf16[4096,64]{0,1:T(8,128)(2,1)S(1)}, bf16[8,512,64]{1,2,0:T(8,128)(2,1)S(1)}, ...), branch_computations={%region_14.14_spmd, %region_15.15_spmd} | conditional | flops 1363805184 | bytes 62908600 | solution.py:241
  677.1 152.7 %reduce-scatter.9.cloned.1.call-done = bf16[512,128]{0,1:T(8,128)(2,1)} async-done(((bf16[4096,128]{0,1:T(8,128)(2,1)}), bf16[512,128]{0,1:T(8,128)(2,1)}) %reduce-scatter.9.cloned.1.call-update) | async-done | bytes 131088 | tf_op jit(solution)/shard_map/reduce_scatter | solution.py:246
  847.8 8.0 convolution_convert_fusion.2
  855.9 8.0 convolution_convert_fusion.1
  864.4 7.8 convolution_convert_fusion
  872.2 8.0 convolution_convert_fusion.6
  884.7 9.2 reduce-scatter.17.cloned.1.call-done
  893.8 34.6 %reduce-scatter.11.cloned.1.call-done = bf16[1024,512]{1,0:T(8,128)(2,1)} async-done(((bf16[2048,512]{1,0:T(8,128)(2,1)}), bf16[1024,512]{1,0:T(8,128)(2,1)}) %reduce-scatter.11.cloned.1.call-update) | async-done | bytes 1048592 | tf_op jit(solution)/shard_map/reduce_scatter | solution.py:292
  928.4 74.4 %reduce-scatter.19.cloned.1.call-done = bf16[1024,1408]{1,0:T(8,128)(2,1)} async-done(((bf16[2048,1408]{1,0:T(8,128)(2,1)}), bf16[1024,1408]{1,0:T(8,128)(2,1)}) %reduce-scatter.19.cloned.1.call-update) | async-done | bytes 2883600 | tf_op jit(solution)/shard_map/reduce_scatter | solution.py:301
  1002.8 74.2 %reduce-scatter.21.cloned.1.call-done = bf16[1024,1408]{1,0:T(8,128)(2,1)} async-done(((bf16[2048,1408]{1,0:T(8,128)(2,1)}), bf16[1024,1408]{1,0:T(8,128)(2,1)}) %reduce-scatter.21.cloned.1.call-update) | async-done | bytes 2883600 | tf_op jit(solution)/shard_map/reduce_scatter | solution.py:304
  1077.0 74.2 %reduce-scatter.23.cloned.1.call-done = bf16[1408,1024]{1,0:T(8,128)(2,1)} async-done(((bf16[1408,2048]{1,0:T(8,128)(2,1)}), bf16[1408,1024]{1,0:T(8,128)(2,1)}) %reduce-scatter.23.cloned.1.call-update) | async-done | bytes 2883600 | tf_op jit(solution)/shard_map/reduce_scatter | solution.py:310
  1153.1 156.0 %all-reduce.12.cloned.1.call-done = (bf16[512,2048]{1,0:T(8,128)(2,1)}, bf16[512,2048]{1,0:T(8,128)(2,1)}) async-done(((bf16[512,2048]{1,0:T(8,128)(2,1)}, bf16[512,2048]{1,0:T(8,128)(2,1)}), (bf16[512,2048]{1,0:T(8,128)(2,1)}, bf16[512,2048]{1,0:T(8,128)(2,1)})) %all-reduce.12.cloned.1.call-update) | async-done | bytes 4194320 | tf_op jit(solution)/shard_map/psum | solution.py:158
  1324.9 7.8 fusion.54
  1332.8 173.9 %all-reduce.14.cloned.1.call-done = (bf16[1024,512]{1,0:T(8,128)(2,1)}, bf16[1024,64]{0,1:T(8,128)(2,1)}, bf16[1024,64]{0,1:T(8,128)(2,1)}, bf16[512,1024]{1,0:T...) async-done(((bf16[1024,512]{1,0:T(8,128)(2,1)}, bf16[1024,64]{0,1:T(8,128)(2,1)}, bf16[1024,64]{0,1:T(8,128)(2,1)}, ...) | async-done | bytes 11010064 | tf_op jit(solution)/shard_map/psum | solution.py:317
  (230 shorter events, 131.1 us)
Async XLA Ops:
  7.2 26.4 %copy-start.1 = (bf16[512,2048]{1,0:T(8,128)(2,1)S(1)}, bf16[512,2048]{1,0:T(8,128)(2,1)}, u32[]{:S(2)}) copy-start(bf16[512,2048]{1,0:T(8,128)(2,1)} %param.19) | copy-start | bytes 6291460
  7.2 9.2 copy-start.26
  7.2 16.7 %copy-start.27 = (bf16[1024,64]{0,1:T(8,128)(2,1)S(1)}, bf16[1024,64]{0,1:T(8,128)(2,1)}, u32[]{:S(2)}) copy-start(bf16[1024,64]{0,1:T(8,128)(2,1)} %param.22) | copy-start | bytes 393220
  7.2 70.0 %all-gather.9.cloned.1.call-start = ((), (), s32[]{:S(2)}) async-start(), calls=%async_computation.8 | async-start | bytes 3145728 | tf_op jit(solution)/shard_map/all_gather | solution.py:68
  7.9 89.4 %all-gather.11.cloned.1.call-start = ((), (), s32[]{:S(2)}) async-start(), calls=%async_computation.9 | async-start | bytes 3145728 | tf_op jit(solution)/shard_map/all_gather | solution.py:73
  8.7 297.7 %all-gather.19.cloned.1.call-start = ((), (), s32[]{:S(2)}) async-start(), calls=%async_computation.22 | async-start | bytes 10485760 | tf_op jit(solution)/shard_map/all_gather | solution.py:147
  8.8 67.5 %copy-start.34 = (f32[32]{0:T(128)}, f32[32]{0:T(128)S(1)}, u32[]{:S(2)}) copy-start(f32[32]{0:T(128)S(1)} %multiply_power_fusion) | copy-start | bytes 388
  8.8 67.5 %copy-start.30 = (f32[512]{0:T(512)}, f32[512]{0:T(512)S(1)}, u32[]{:S(2)}) copy-start(f32[512]{0:T(512)S(1)} %fusion.91) | copy-start | bytes 6148
  14.3 20.6 %copy-start.24 = (f32[2048]{0:T(1024)}, f32[2048]{0:T(1024)S(1)}, u32[]{:S(2)}) copy-start(f32[2048]{0:T(1024)S(1)} %convert_element_type.202) | copy-start | bytes 24580
  16.4 18.8 %copy-start.32 = (f32[512]{0:T(512)}, f32[512]{0:T(512)S(1)}, u32[]{:S(2)}) copy-start(f32[512]{0:T(512)S(1)} %add_rsqrt_fusion.1) | copy-start | bytes 6148
  23.9 30.9 %copy-start.12 = (bf16[2048,64]{0,1:T(8,128)(2,1)}, bf16[2048,64]{0,1:T(8,128)(2,1)S(1)}, u32[]{:S(2)}) copy-start(bf16[2048,64]{0,1:T(8,128)(2,1)S(1)} %all_gather.51) | copy-start | bytes 786436
  32.9 21.9 %copy-start.14 = (bf16[2048,64]{0,1:T(8,128)(2,1)}, bf16[2048,64]{0,1:T(8,128)(2,1)S(1)}, u32[]{:S(2)}) copy-start(bf16[2048,64]{0,1:T(8,128)(2,1)S(1)} %all_gather.54) | copy-start | bytes 786436
  34.1 19.9 %copy-start.2 = (bf16[512,2048]{1,0:T(8,128)(2,1)}, bf16[512,2048]{1,0:T(8,128)(2,1)S(1)}, u32[]{:S(2)}) copy-start(bf16[512,2048]{1,0:T(8,128)(2,1)S(1)} %fusion.59) | copy-start | bytes 6291460
  101.8 278.6 %all-gather.13.cloned.1.call-start = ((), (), s32[]{:S(2)}) async-start(), calls=%async_computation.10 | async-start | bytes 8650752 | tf_op jit(solution)/shard_map/all_gather | solution.py:71
  102.4 353.9 %all-gather.15.cloned.1.call-start = ((), (), s32[]{:S(2)}) async-start(), calls=%async_computation.11 | async-start | bytes 8650752 | tf_op jit(solution)/shard_map/all_gather | solution.py:72
  102.9 429.2 %all-gather.17.cloned.1.call-start = ((), (), s32[]{:S(2)}) async-start(), calls=%async_computation.12 | async-start | bytes 8650752 | tf_op jit(solution)/shard_map/all_gather | solution.py:74
  103.5 536.8 %all-reduce.10.cloned.1.call-start = ((), (), s32[]{:S(2)}) async-start(), calls=%async_computation.13 | async-start | bytes 4194304 | tf_op jit(solution)/shard_map/psum | solution.py:182
  554.0 275.8 %reduce-scatter.9.cloned.1.call-start = ((), (), s32[]{:S(2)}) async-start(), calls=%async_computation.14 | async-start | bytes 1179648 | tf_op jit(solution)/shard_map/reduce_scatter | solution.py:246
  674.1 156.5 %copy-start.31 = (f32[512]{0:T(512)S(1)}, f32[512]{0:T(512)}, u32[]{:S(2)}) copy-start(f32[512]{0:T(512)} %copy-done.30) | copy-start | bytes 6148
  674.2 156.5 %copy-start.35 = (f32[32]{0:T(128)S(1)}, f32[32]{0:T(128)}, u32[]{:S(2)}) copy-start(f32[32]{0:T(128)} %copy-done.34) | copy-start | bytes 388
  676.9 207.7 %reduce-scatter.13.cloned.1.call-start = ((), (), s32[]{:S(2)}) async-start(), calls=%async_computation.16 | async-start | bytes 393216 | tf_op jit(solution)/shard_map/reduce_scatter | solution.py:295
  833.8 50.8 %reduce-scatter.15.cloned.1.call-start = ((), (), s32[]{:S(2)}) async-start(), calls=%async_computation.17 | async-start | bytes 393216 | tf_op jit(solution)/shard_map/reduce_scatter | solution.py:298
  836.8 57.1 %reduce-scatter.17.cloned.1.call-start = ((), (), s32[]{:S(2)}) async-start(), calls=%async_computation.18 | async-start | bytes 3145728 | tf_op jit(solution)/shard_map/reduce_scatter | solution.py:307
  843.4 85.0 %reduce-scatter.11.cloned.1.call-start = ((), (), s32[]{:S(2)}) async-start(), calls=%async_computation.15 | async-start | bytes 3145728 | tf_op jit(solution)/shard_map/reduce_scatter | solution.py:292
  847.8 155.0 %reduce-scatter.19.cloned.1.call-start = ((), (), s32[]{:S(2)}) async-start(), calls=%async_computation.19 | async-start | bytes 8650752 | tf_op jit(solution)/shard_map/reduce_scatter | solution.py:301
  855.9 221.2 %reduce-scatter.21.cloned.1.call-start = ((), (), s32[]{:S(2)}) async-start(), calls=%async_computation.20 | async-start | bytes 8650752 | tf_op jit(solution)/shard_map/reduce_scatter | solution.py:304
  863.9 287.3 %reduce-scatter.23.cloned.1.call-start = ((), (), s32[]{:S(2)}) async-start(), calls=%async_computation.21 | async-start | bytes 8650752 | tf_op jit(solution)/shard_map/reduce_scatter | solution.py:310
  872.2 437.0 %all-reduce.12.cloned.1.call-start = ((), (), s32[]{:S(2)}) async-start(), calls=%async_computation.23 | async-start | bytes 8388608 | tf_op jit(solution)/shard_map/psum | solution.py:158
  872.2 8.0 copy-start.17
  884.6 622.2 %all-reduce.14.cloned.1.call-start = ((), (), s32[]{:S(2)}) async-start(), calls=%async_computation.24 | async-start | bytes 22020096 | tf_op jit(solution)/shard_map/psum | solution.py:317
  1151.2 157.9 %copy-start.25 = (f32[2048]{0:T(1024)S(1)}, f32[2048]{0:T(1024)}, u32[]{:S(2)}) copy-start(f32[2048]{0:T(1024)} %copy-done.24) | copy-start | bytes 24580
  1151.2 157.9 %copy-start.33 = (f32[512]{0:T(512)S(1)}, f32[512]{0:T(512)}, u32[]{:S(2)}) copy-start(f32[512]{0:T(512)} %copy-done.32) | copy-start | bytes 6148
  (27 other events, 84.1 us)
Sparse Core Ops, SparseCore 0:
  9.6 40.0 all-gather.8
  51.2 36.7 all-gather.10
  101.9 204.4 all-gather.18
  307.8 72.6 all-gather.12
  381.8 74.4 all-gather.14
  457.7 74.4 all-gather.16
  554.2 86.1 all-reduce.9
  677.0 152.7 reduce-scatter.8
  834.0 11.7 reduce-scatter.12
  847.8 11.7 reduce-scatter.14
  861.9 31.8 reduce-scatter.16
  896.5 31.8 reduce-scatter.10
  931.3 71.4 reduce-scatter.18
  1005.5 71.4 reduce-scatter.20
  1079.7 71.4 reduce-scatter.22
  1154.1 155.0 all-reduce.11
  1312.2 194.4 all-reduce.13
